TPU v7x, 32 devices: a whole 2x2x4 slice. The times are simulated.
32 devices in a mesh: client: 32 (over z, y, x, core).
Axes of the slice: x: 2, y: 2, z: 4, core: 2. Of those that a mesh axis runs over, the one named last changes fastest.
Arguments:
- patches: bfloat16 [4096, 192], P('client'), may hold values from -6 to 6
- labels: int32 [256], replicated, may hold values from 0 to 9
- assign: int32 [32, 1], replicated, may hold values from 0 to 15; in each aligned block of 32 rows (0 to 31, 32 to 63, ...) at most 4 rows name the same one
- patch_embed: bfloat16 [192, 384], replicated, may hold values from -0.4375 to 0.4375
- positions: bfloat16 [16, 384], replicated, may hold values from -3 to 3
- client_in: bfloat16 [384, 3072], replicated, may hold values from -3 to 3
- client_down: bfloat16 [1536, 384], replicated, may hold values from -0.15625 to 0.15625
- server_in: bfloat16 [2, 6144, 3072], P(None, 'client'), may hold values from -3 to 3
- server_down: bfloat16 [2, 24576, 384], P(None, 'client'), may hold values from -0.15625 to 0.15625
- classifier: bfloat16 [16, 384, 10], replicated, may hold values from -15 to 15
Outputs:
- losses: float32 [32, 16], P('client')
- grad_patch_embed: float32 [192, 384], P(None, 'client')
- grad_positions: float32 [16, 384], P(None, 'client')
- grad_client_in: float32 [384, 3072], P(None, 'client')
- grad_client_down: float32 [1536, 384], P(None, 'client')
- grad_server_in: float32 [2, 6144, 3072], P(None, 'client')
- grad_server_down: float32 [2, 24576, 384], P(None, 'client')
- grad_classifier: float32 [6144, 10], P('client')
Inputs may be any that keep to these rules, and one draw needn't show every extreme that they name: `assign`: no server shard is named by more than 4 clients, a bound that some block reaches.
All inputs are finite; a program needn't handle non-finite values.
Results may differ from a plain program's by a relative error of at most 0.025.
Values may be sent and summed in bfloat16 or wider, within the bound.
No kernel may reach another device: no remote copies, remote signals or barrier semaphores. Data moves between devices by JAX's collectives and lax.ppermute only.
A program may use at most 128 MiB of HBM per device.

v0:
```python
import math

import jax
import jax.numpy as jnp
from jax import lax
from jax.experimental import pallas as pl
from jax.experimental.pallas import tpu as pltpu
from jax.sharding import PartitionSpec as P


HEADS = 6
SHARDS = 16
SLOTS = 2
EPSILON = 1e-06
BF = jnp.bfloat16
F32 = jnp.float32
GELU_A = math.sqrt(2.0 / math.pi)
GELU_B = 0.044715
LANES = 128
ROWS16 = 16


def mm(a, b):
    return lax.dot_general(a, b, (((1,), (0,)), ((), ())), preferred_element_type=F32)


def mm_nt(a, b):
    return lax.dot_general(a, b, (((1,), (1,)), ((), ())), preferred_element_type=F32)


def mm_tn(a, b):
    return lax.dot_general(a, b, (((0,), (0,)), ((), ())), preferred_element_type=F32)


def norm_forward(x):
    centre = x - jnp.mean(x, axis=-1, keepdims=True)
    spread = jnp.mean(centre * centre, axis=-1, keepdims=True)
    scale = lax.rsqrt(spread + EPSILON)
    return centre * scale, scale


def norm_backward(grad, normed, scale):
    mean_grad = jnp.mean(grad, axis=-1, keepdims=True)
    mean_both = jnp.mean(grad * normed, axis=-1, keepdims=True)
    return scale * (grad - mean_grad - normed * mean_both)


PIECES = 2


def stage_orders(bits, piece):
    if bits == 5:
        return (((1, 2, 3, 4), (2, 3, 1, 4)), ((3, 1, 2, 4), (3, 1, 2, 4)))[piece]
    *turning, last = range(1, bits)
    third = max(1, len(turning) // 3)
    turns = [tuple(turning[i * third :] + turning[: i * third]) + (last,) for i in range(3)]
    return ((turns[0], turns[1]), (turns[2], turns[2]))[piece]


def slot_of_chip(offset, core, bits, piece):
    def place(order):
        value = 0
        for step, bit in enumerate(order):
            value = value | (((offset >> (bit - 1)) & 1) << (bits - 2 - step))
        return value

    even, odd = stage_orders(bits, piece)
    return place(even) if even == odd else jnp.where(core == 0, place(even), place(odd))


def split_rows(x, mask):
    return jnp.concatenate([jnp.where(mask, x, 0.0), jnp.where(mask, 0.0, x)], axis=0)


def compact(stacked, images, tok, lane_image):
    value = stacked[:tok]
    for i in range(1, images):
        value = jnp.where(lane_image == i, stacked[i * tok : (i + 1) * tok], value)
    return value


def expand(value, images, lane_image):
    return jnp.concatenate([jnp.where(lane_image == i, value, 0.0) for i in range(images)], axis=0).astype(BF)


def make_chain(cfg):
    d, ff, tok = cfg["d"], cfg["ff"], cfg["tok"]
    members, group, capacity, pr = cfg["members"], cfg["group"], cfg["capacity"], cfg["pr"]
    images, classes, patch = cfg["images"], cfg["classes"], cfg["patch"]
    layers, bits = cfg["layers"], cfg["bits"]
    rows = capacity * pr
    per_image = pr // tok
    rows_in, rows_down, pieces = d // group, ff // group, cfg["pieces"]
    cin, cin_pad = cfg["cin"], cfg["cin_pad"]
    chips = members // 2
    halves = rows // LANES
    pairs = d // LANES
    dpc = d // members
    chunk = d
    heights = cfg["heights"]
    packed = cfg["packed"]

    def kernel(*refs):
        (assign, labels, arrived, embed_hbm, positions_hbm, client_in, client_down), refs = refs[:7], refs[7:]
        piece_in, refs = refs[: len(pieces)], refs[len(pieces) :]
        piece_down, refs = refs[: len(pieces)], refs[len(pieces) :]
        classifier_hbm, refs = refs[0], refs[1:]
        (losses, dcls), refs = refs[:2], refs[2:]
        grads, refs = refs[: 2 * PIECES], refs[2 * PIECES :]
        saved_out, refs = refs[:8], refs[8:]
        (w_in, w_down, slot, x_ref, y_ref, qkv_f, qkv_b, prob, gp, r1, r2), refs = refs[:11], refs[11:]
        (score, spread, dspread, embed, classifier), refs = refs[:5], refs[5:]
        saved_refs = refs[:8]
        (c_u, c_o, c_u2, c_h, c_dqkv, c_dy, c_dpre, c_dout, pcat, dob_pad), refs = refs[:10], refs[10:]
        (sems,) = refs

        me = lax.axis_index("client")
        rank = me % group
        shard = me // group
        core = me % 2

        def weight_copies(layer, half):
            if layer == 0:
                wanted = ((pl.ds(0, 4 * d), 0),) if half == 0 else ((pl.ds(4 * d, ff), 1),)
                out = [
                    pltpu.make_async_copy(client_in.at[:, cols], w_in.at[0, :, cols], sems.at[sem])
                    for cols, sem in wanted
                ]
                if half == 1:
                    out.append(pltpu.make_async_copy(client_down, w_down.at[0], sems.at[2]))
                return out
            base = 3 + (layer - 1) * 2 * group + half
            sources, target, height = (
                (piece_in, w_in, rows_in) if half == 0 else (piece_down, w_down, rows_down)
            )
            out = []
            for source, start, count in zip(sources, cfg["first"], pieces):
                for inner in range(count):
                    index = start + inner
                    at = pl.ds(pl.multiple_of((rank ^ index) * height, height), height)
                    out.append(
                        pltpu.make_async_copy(
                            source.at[inner, layer - 1], target.at[layer, at], sems.at[base + 2 * index]
                        )
                    )
            return out

        first_other = 3 + (layers - 1) * 2 * group

        def saved_copies(layer):
            base = first_other + (layer - 1) * 8
            return [
                pltpu.make_async_copy(src.at[layer], dst.at[layer - 1], sems.at[base + i])
                for i, (src, dst) in enumerate(zip(saved_refs, saved_out))
            ]

        last_sem = first_other + (layers - 1) * 8
        small = [
            pltpu.make_async_copy(embed_hbm, embed.at[pl.ds(0, patch)], sems.at[last_sem]),
            pltpu.make_async_copy(positions_hbm, embed.at[pl.ds(patch, tok)], sems.at[last_sem + 1]),
        ]
        cls_copy = pltpu.make_async_copy(classifier_hbm, classifier, sems.at[last_sem + 2])
        for copy in small:
            copy.start()
        for half in range(2):
            for copy in weight_copies(0, half):
                copy.start()
        cls_copy.start()
        for k in range(capacity):
            slot[k] = 0

        def scan(c, count):
            hit = (assign[c] == shard) & (count < capacity)

            @pl.when(hit)
            def _():
                slot[count] = c

            return count + hit.astype(jnp.int32)

        filled = lax.fori_loop(0, members, scan, jnp.int32(0))
        half_mask = lax.broadcasted_iota(jnp.int32, (LANES, LANES), 1) < LANES // 2
        width_slot = LANES // group
        lane = lax.broadcasted_iota(jnp.int32, (packed, LANES), 1)
        for v in range(halves):
            blocks = [arrived[slot[v * group + t]].astype(F32) for t in range(group)]
            for part in range(group):
                value = blocks[0]
                for t in range(group):
                    moved = pltpu.roll(blocks[t], (width_slot * (t - part)) % LANES, 1)
                    value = jnp.where(lane // width_slot == t, moved, value)
                pcat[part * packed : (part + 1) * packed, v * LANES : (v + 1) * LANES] = value.astype(BF)
        token = lax.broadcasted_iota(jnp.int32, (tok, rows), 1) % tok
        pcat[patch:] = (token == lax.broadcasted_iota(jnp.int32, (tok, rows), 0)).astype(F32).astype(BF)
        for copy in small:
            copy.wait()
        x_ref[...] = mm_tn(pcat[...], embed[...])

        row_slot = lax.broadcasted_iota(jnp.int32, (rows, 1), 0) // pr
        group_images = LANES // tok
        lane_image = lax.broadcasted_iota(jnp.int32, (tok, LANES), 1) // tok

        def forward(layer, carry):
            for which in range(layers):

                @pl.when(layer == which)
                def _(which=which):
                    for copy in weight_copies(which, 0):
                        copy.wait()
                    if which == 0:
                        for later in range(1, layers):
                            for half in range(2):
                                for copy in weight_copies(later, half):
                                    copy.start()

            x = x_ref[...]
            normed, scale = norm_forward(x)
            u = normed.astype(BF)
            c_u[layer] = u
            r1[layer] = scale
            for part in range(3):
                value = mm(u, w_in[layer, :, part * d : (part + 1) * d])
                qkv_f[:, part * d : (part + 1) * d] = value
                qkv_b[layer, :, part * d : (part + 1) * d] = value.astype(BF)
            head_dim = d // HEADS
            tiles = [(g, p) for g in range(halves) for p in range(pairs)]
            for number, (g, p) in enumerate(tiles):
                rs = slice(g * LANES, (g + 1) * LANES)
                q = qkv_f[rs, p * LANES : (p + 1) * LANES] * (1.0 / math.sqrt(head_dim))
                k = qkv_f[rs, d + p * LANES : d + (p + 1) * LANES]
                k2 = split_rows(k, half_mask)
                k_hi = k2.astype(BF)
                k_lo = (k2 - k_hi.astype(F32)).astype(BF)
                q_hi = q.astype(BF)
                q_lo = (q - q_hi.astype(F32)).astype(BF)
                score[number] = mm_nt(
                    jnp.concatenate([k_hi, k_lo], 1), jnp.concatenate([q_hi, q_hi], 1)
                ) + mm_nt(k_hi, q_lo)
            for number in range(len(tiles)):
                for j in range(2):
                    part = compact(score[number, j * LANES : (j + 1) * LANES], group_images, tok, lane_image)
                    e = jnp.exp(part - jnp.max(part, axis=0, keepdims=True))
                    weight = e / jnp.sum(e, axis=0, keepdims=True)
                    prob[layer, 2 * number + j] = weight
                    spread[number, j * LANES : (j + 1) * LANES] = expand(weight, group_images, lane_image)
            for number, (g, p) in enumerate(tiles):
                rs = slice(g * LANES, (g + 1) * LANES)
                v = qkv_f[rs, 2 * d + p * LANES : 2 * d + (p + 1) * LANES]
                o = mm_tn(spread[number], split_rows(v, half_mask).astype(BF))
                c_o[layer, rs, p * LANES : (p + 1) * LANES] = o.astype(BF)
            for which in range(layers):

                @pl.when(layer == which)
                def _(which=which):
                    for copy in weight_copies(which, 1):
                        copy.wait()

            y = x_ref[...] + mm(c_o[layer], w_in[layer, :, 3 * d : 4 * d])
            y_ref[...] = y
            normed, scale = norm_forward(y)
            u2 = normed.astype(BF)
            c_u2[layer] = u2
            r2[layer] = scale
            for part in range(ff // chunk):
                cs = slice(part * chunk, (part + 1) * chunk)
                pre = mm(u2, w_in[layer, :, 4 * d + part * chunk : 4 * d + (part + 1) * chunk])
                square = pre * pre
                t = jnp.tanh(pre * (GELU_A + (GELU_A * GELU_B) * square))
                half = 0.5 * t + 0.5
                hidden = pre * half
                c_h[layer, :, cs] = hidden.astype(BF)
                slope = half + hidden * ((1.0 - half) * (2.0 * GELU_A + (6.0 * GELU_A * GELU_B) * square))
                gp[layer, :, cs] = slope.astype(BF)
            x_ref[...] = y_ref[...] + mm(c_h[layer], w_down[layer])

            @pl.when(layer == 0)
            def _():
                cut = x_ref[...].astype(BF).astype(F32)
                x_ref[...] = jnp.where(row_slot < filled, cut, 0.0)

            return carry

        lax.fori_loop(0, layers, forward, 0)

        cls_copy.wait()
        pooled = jnp.mean(x_ref[...].reshape(images, tok, d), axis=1)
        pnorm, pscale = norm_forward(pooled)
        pb = pnorm.astype(BF)
        here = lax.broadcasted_iota(jnp.int32, classifier.shape, 1) == shard
        weights_cls = jnp.sum(jnp.where(here, classifier[...].astype(F32), 0.0), axis=1).astype(BF)
        logits = mm_nt(pb, weights_cls)
        image = lax.broadcasted_iota(jnp.int32, (images, 1), 0)
        label = jnp.zeros((images, 1), jnp.int32)
        for n in range(images):
            k, i = n // per_image, n % per_image
            value = labels[slot[k] * cfg["img"] + rank * per_image + i]
            label = jnp.where(image == n, value, label)
        full = (image // per_image < filled).astype(F32)
        hot = (lax.broadcasted_iota(jnp.int32, (images, classes), 1) == label).astype(F32)
        top = jnp.max(logits, axis=1, keepdims=True)
        e = jnp.exp(logits - top)
        total = jnp.sum(e, axis=1, keepdims=True)
        picked = jnp.sum(hot * logits, axis=1, keepdims=True)
        loss = (jnp.log(total) + top - picked) * full
        diagonal = lax.broadcasted_iota(jnp.int32, (images, images), 1) == image
        losses[...] = jnp.sum(jnp.where(diagonal, loss, 0.0), axis=0, keepdims=True)
        dlogits = ((e / total - hot) * full).astype(BF)
        dcls[...] = mm_tn(dlogits, pb)
        dpb = mm(dlogits, weights_cls).astype(BF).astype(F32)
        dpool = norm_backward(dpb, pnorm, pscale) * (1.0 / tok)
        x_ref[...] = jnp.broadcast_to(dpool[:, None, :], (images, tok, d)).reshape(rows, d)

        def backward(step, carry):
            layer = layers - 1 - step
            dout = x_ref[...]
            dob = dout.astype(BF)
            c_dout[layer] = dob
            for part in range(ff // chunk):
                cs = slice(part * chunk, (part + 1) * chunk)
                dh = mm_nt(dob, w_down[layer, cs]).astype(BF).astype(F32)
                c_dpre[layer, :, cs] = (dh * gp[layer, :, cs].astype(F32)).astype(BF)
            du2 = mm_nt(c_dpre[layer], w_in[layer, :, 4 * d :]).astype(BF).astype(F32)
            dy = x_ref[...] + norm_backward(du2, c_u2[layer].astype(F32), r2[layer])
            y_ref[...] = dy
            dyb = dy.astype(BF)
            c_dy[layer] = dyb
            do = mm_nt(dyb, w_in[layer, :, 3 * d : 4 * d]).astype(BF)
            head_dim = d // HEADS
            tiles = [(g, p) for g in range(halves) for p in range(pairs)]
            qkv_f[:, :d] = do.astype(F32)
            for number, (g, p) in enumerate(tiles):
                rs, ls = slice(g * LANES, (g + 1) * LANES), slice(p * LANES, (p + 1) * LANES)
                v = qkv_b[layer, rs, 2 * d + p * LANES : 2 * d + (p + 1) * LANES].astype(F32)
                score[number] = mm_nt(split_rows(v, half_mask).astype(BF), qkv_f[rs, ls].astype(BF))
            for number in range(len(tiles)):
                for j in range(2):
                    weight = prob[layer, 2 * number + j]
                    part = compact(score[number, j * LANES : (j + 1) * LANES], group_images, tok, lane_image)
                    mixed = weight * part
                    dscore = mixed - weight * jnp.sum(mixed, axis=0, keepdims=True)
                    spread[number, j * LANES : (j + 1) * LANES] = expand(weight, group_images, lane_image)
                    dspread[number, j * LANES : (j + 1) * LANES] = expand(
                        dscore * (1.0 / math.sqrt(head_dim)), group_images, lane_image
                    )
            for number, (g, p) in enumerate(tiles):
                rs, ls = slice(g * LANES, (g + 1) * LANES), slice(p * LANES, (p + 1) * LANES)
                d2 = split_rows(qkv_f[rs, ls], half_mask).astype(BF)
                q = qkv_b[layer, rs, p * LANES : (p + 1) * LANES].astype(F32)
                k = qkv_b[layer, rs, d + p * LANES : d + (p + 1) * LANES].astype(F32)
                wide = jnp.concatenate([spread[number, :LANES], spread[number, LANES:]], 1)
                dwide = jnp.concatenate([dspread[number, :LANES], dspread[number, LANES:]], 1)
                dv = mm(wide, d2)
                dk = mm(dwide, split_rows(q, half_mask).astype(BF))
                dq = mm_tn(dspread[number], split_rows(k, half_mask).astype(BF))
                c_dqkv[layer, rs, p * LANES : (p + 1) * LANES] = dq.astype(BF)
                c_dqkv[layer, rs, d + p * LANES : d + (p + 1) * LANES] = dk.astype(BF)
                c_dqkv[layer, rs, 2 * d + p * LANES : 2 * d + (p + 1) * LANES] = dv.astype(BF)
            du = mm_nt(c_dqkv[layer], w_in[layer, :, : 3 * d]).astype(BF).astype(F32)
            dx = y_ref[...] + norm_backward(du, c_u[layer].astype(F32), r1[layer])
            x_ref[...] = dx

            @pl.when(layer == 1)
            def _():
                x_ref[...] = x_ref[...].astype(BF).astype(F32)

            for which in range(1, layers):

                @pl.when(layer == which)
                def _(which=which):
                    for copy in saved_copies(which):
                        copy.start()

            return carry

        lax.fori_loop(0, layers, backward, 0)

        chip = me // 2

        def emit(values, piece, at):
            for n in sorted(values)[::2]:
                own = jnp.where(core == 0, values[n], values[n + 1])
                other = jnp.where(core == 0, values[n + 1], values[n])
                offset = chip ^ (n // 2)
                grads[2 * piece][slot_of_chip(offset, core, bits, piece), at] = own.astype(BF)
                grads[2 * piece + 1][slot_of_chip(offset, 1 - core, bits, piece), at] = other.astype(BF)

        copies = []
        for layer in range(1, layers):
            copies += saved_copies(layer)

        def emit_columns(first, cot, act):
            value = mm_tn(cot, act)
            count = value.shape[0] // cin
            base = first // cin
            emit({base + i: value[i * cin : (i + 1) * cin] for i in range(count)}, 0, slice(0, cin))

        for part in range(3):
            emit_columns(part * d, c_dqkv[0, :, part * d : (part + 1) * d], c_u[0])
        emit_columns(3 * d, c_dy[0], c_o[0])
        for part in range(ff // d):
            emit_columns(4 * d + part * d, c_dpre[0, :, part * d : (part + 1) * d], c_u2[0])
        width = members * ROWS16
        column = lax.broadcasted_iota(jnp.int32, (d, width), 1)
        row = lax.broadcasted_iota(jnp.int32, (d, width), 0)
        inner = column % ROWS16
        sel = ((inner < dpc) & (row == (column // ROWS16) * dpc + inner)).astype(BF)
        dob_pad[...] = mm(x_ref[...].astype(BF), sel).astype(BF)
        extra = jnp.concatenate([mm(pcat[...], dob_pad[...]), jnp.zeros((d - patch - tok, width), F32)], 0).T
        dob_pad[...] = mm(c_dout[0], sel).astype(BF)
        parts = ff // d
        share = -(-dpc // parts)
        out_row = lax.broadcasted_iota(jnp.int32, (width, d), 0) % ROWS16
        for part in range(parts):
            value = mm_tn(dob_pad[...], c_h[0, :, part * d : (part + 1) * d])
            moved = pltpu.roll(extra, (dpc - share * part) % width, 0)
            value = jnp.where((out_row >= dpc) & (out_row < dpc + share), moved, value)
            emit(
                {n: value[n * ROWS16 : (n + 1) * ROWS16] for n in range(members)},
                0 if part == 0 else 1,
                slice(cin_pad, cin_pad + ROWS16) if part == 0 else slice((part - 1) * ROWS16, part * ROWS16),
            )
        for copy in copies:
            copy.wait()

    wide = 4 * d + ff
    saved = [d, d, d, ff, 3 * d, d, ff, d]
    out_shape = [
        jax.ShapeDtypeStruct((1, images), F32),
        jax.ShapeDtypeStruct((classes, d), F32),
    ] + [jax.ShapeDtypeStruct((chips, height, d), BF) for height in heights for _ in range(2)]
    out_shape = out_shape + [pltpu.HBM((layers - 1, rows, w), BF) for w in saved]
    any_spec = pl.BlockSpec(memory_space=pl.ANY)
    hbm = pl.BlockSpec(memory_space=pltpu.HBM)
    smem = pl.BlockSpec(memory_space=pltpu.SMEM)
    vmem = pl.BlockSpec(memory_space=pltpu.VMEM)
    n_sems = 3 + (layers - 1) * 2 * group + (layers - 1) * 8 + 3
    scratch = [
        pltpu.VMEM((layers, d, wide), BF),
        pltpu.VMEM((layers, ff, d), BF),
        pltpu.SMEM((capacity,), jnp.int32),
        pltpu.VMEM((rows, d), F32),
        pltpu.VMEM((rows, d), F32),
        pltpu.VMEM((rows, 3 * d), F32),
        pltpu.VMEM((layers, rows, 3 * d), BF),
        pltpu.VMEM((layers, halves * pairs * 2, tok, LANES), F32),
        pltpu.VMEM((layers, rows, ff), BF),
        pltpu.VMEM((layers, rows, 1), F32),
        pltpu.VMEM((layers, rows, 1), F32),
        pltpu.VMEM((halves * pairs, 2 * LANES, LANES), F32),
        pltpu.VMEM((halves * pairs, 2 * LANES, LANES), BF),
        pltpu.VMEM((halves * pairs, 2 * LANES, LANES), BF),
        pltpu.VMEM((patch + tok, d), BF),
        pltpu.VMEM((classes, members // group, d), BF),
    ]
    scratch += [pltpu.VMEM((layers, rows, w), BF) for w in saved]
    scratch += [
        pltpu.VMEM((patch + tok, rows), BF),
        pltpu.VMEM((rows, members * ROWS16), BF),
    ]
    scratch += [
        pltpu.SemaphoreType.DMA((n_sems,)),
    ]
    return pl.pallas_call(
        kernel,
        name="chain",
        in_specs=[smem, smem, vmem] + [hbm] * (5 + 2 * len(pieces)),
        out_specs=[vmem] * (2 + 2 * PIECES) + [hbm] * (len(out_shape) - 2 - 2 * PIECES),
        out_shape=out_shape,
        scratch_shapes=scratch,
        compiler_params=pltpu.CompilerParams(vmem_limit_bytes=cfg['vmem']),
    )


def make_pack(cfg):
    members, group, patch = cfg["members"], cfg["group"], cfg["patch"]
    packed, width = patch // group, LANES // group

    def kernel(patches, out):
        lane = lax.broadcasted_iota(jnp.int32, (packed, LANES), 1)
        parts = [patches[s * packed : (s + 1) * packed].astype(F32) for s in range(group)]
        for j in range(group):
            value = parts[0]
            for s in range(group):
                moved = pltpu.roll(parts[s], (width * (s - j)) % LANES, 1)
                value = jnp.where(lane // width == s, moved, value)
            value = value.astype(BF)
            for shard in range(members // group):
                out[shard * group + j] = value

    return pl.pallas_call(
        kernel,
        name="pack",
        out_shape=jax.ShapeDtypeStruct((members, packed, LANES), BF),
    )


def make_stage(shapes):
    count = len(shapes)

    def kernel(*refs):
        sources, targets, sems = refs[:count], refs[count : 2 * count], refs[2 * count]
        copies = [pltpu.make_async_copy(sources[i], targets[i], sems.at[i]) for i in range(count)]
        for copy in copies:
            copy.start()
        for copy in copies:
            copy.wait()

    return pl.pallas_call(
        kernel,
        name="stage",
        in_specs=[pl.BlockSpec(memory_space=pl.ANY)] * count,
        out_specs=[pl.BlockSpec(memory_space=pltpu.HBM)] * count,
        out_shape=[pltpu.HBM(shape, BF) for shape in shapes],
        scratch_shapes=[pltpu.SemaphoreType.DMA((count,))],
    )


def make_server_grads(cfg):
    d, ff, group, layers = cfg["d"], cfg["ff"], cfg["group"], cfg["layers"]
    rows_in, rows_down = d // group, ff // group
    wide = 4 * d + ff
    half = group // 2
    count = layers - 1
    rows = cfg["capacity"] * cfg["pr"]
    saved = [d, d, d, ff, 3 * d, d, ff, d]

    def kernel(*refs):
        sources, refs = refs[:8], refs[8:]
        k_in, s_in, k_down, s_down = refs[:4]
        local, t_in, t_down, sems = refs[4:12], refs[12], refs[13], refs[14]
        rank = lax.axis_index("client") % group

        def loads(layer):
            return [
                pltpu.make_async_copy(src.at[layer], dst.at[layer], sems.at[8 * layer + i])
                for i, (src, dst) in enumerate(zip(sources, local))
            ]

        def stores(layer):
            out = []
            for p in range(group):
                owner = rank ^ p
                o_in, o_down = (k_in, k_down) if p < half else (s_in, s_down)
                at_in = pl.ds(pl.multiple_of(owner * rows_in, rows_in), rows_in)
                at_down = pl.ds(pl.multiple_of(owner * rows_down, rows_down), rows_down)
                sem = 8 * count + 2 * (layer * group + p)
                out.append(pltpu.make_async_copy(t_in.at[layer, at_in], o_in.at[p % half, layer], sems.at[sem]))
                out.append(
                    pltpu.make_async_copy(t_down.at[layer, at_down], o_down.at[p % half, layer], sems.at[sem + 1])
                )
            return out

        for layer in range(count):
            for copy in loads(layer):
                copy.start()

        def compute(layer, carry):
            for which in range(count):

                @pl.when(layer == which)
                def _(which=which):
                    for copy in loads(which):
                        copy.wait()

            u, o, u2, h, dqkv, dy, dpre, dout = [ref.at[layer] for ref in local]
            for part in range(3):
                cs = slice(part * d, (part + 1) * d)
                t_in[layer, :, cs] = mm_tn(u[...], dqkv[:, cs]).astype(BF)
            t_in[layer, :, 3 * d : 4 * d] = mm_tn(o[...], dy[...]).astype(BF)
            for part in range(ff // d):
                cs = slice(part * d, (part + 1) * d)
                t_in[layer, :, 4 * d + part * d : 4 * d + (part + 1) * d] = mm_tn(u2[...], dpre[:, cs]).astype(BF)
                t_down[layer, cs] = mm_tn(h[:, cs], dout[...]).astype(BF)
            for which in range(count):

                @pl.when(layer == which)
                def _(which=which):
                    for copy in stores(which):
                        copy.start()

            return carry

        lax.fori_loop(0, count, compute, 0)
        for layer in range(count):
            for copy in stores(layer):
                copy.wait()

    flops = 2 * rows * (d * wide + ff * d) * count
    any_spec = pl.BlockSpec(memory_space=pl.ANY)
    return pl.pallas_call(
        kernel,
        name="server_grads",
        in_specs=[any_spec] * 8,
        out_specs=[any_spec] * 4,
        out_shape=[jax.ShapeDtypeStruct((half, count, rows_in, wide), BF)] * 2
        + [jax.ShapeDtypeStruct((half, count, rows_down, d), BF)] * 2,
        scratch_shapes=[pltpu.VMEM((count, rows, w), BF) for w in saved]
        + [
            pltpu.VMEM((count, d, wide), BF),
            pltpu.VMEM((count, ff, d), BF),
            pltpu.SemaphoreType.DMA((8 * count + 2 * count * group,)),
        ],
        cost_estimate=pl.CostEstimate(flops=flops * 2, bytes_accessed=16 * 2**20, transcendentals=0),
        compiler_params=pltpu.CompilerParams(vmem_limit_bytes=20 * 1024 * 1024),
    )


def make_finish(cfg):
    d, ff, tok, patch = cfg["d"], cfg["ff"], cfg["tok"], cfg["patch"]
    members, cin, group = cfg["members"], cfg["cin"], cfg["group"]
    classes = cfg["classes"]
    dpc, rows_in = d // members, d // group

    heights, cin_pad = cfg["heights"], cfg["cin_pad"]
    parts = ff // d
    share = -(-dpc // parts)

    def kernel(a0, a1, b, cls, g_embed, g_pos, g_in, g_down, g_class):
        first = a0[0].astype(F32) + b[0, : heights[0]].astype(F32)
        g_in[...] = first[:cin]
        rest = a1[0].astype(F32) + b[0, heights[0] :].astype(F32)
        total = jnp.concatenate([first[cin_pad:], rest], axis=0)
        extra = []
        for part in range(parts):
            block = total[part * ROWS16 : (part + 1) * ROWS16]
            g_down[:, part * d : (part + 1) * d] = block[:dpc]
            if share * part < dpc:
                extra.append(block[dpc : dpc + min(share, dpc - share * part)])
        extra = jnp.concatenate(extra, axis=0)
        g_embed[...] = extra[:, :patch]
        padded = jnp.concatenate([extra[:, patch : patch + tok], jnp.zeros((ROWS16 - dpc, tok), F32)], axis=0)
        g_pos[...] = padded.T[:, :dpc]
        rank = lax.axis_index("client") % group
        value = cls[:, :rows_in]
        for r in range(1, group):
            value = jnp.where(rank == r, cls[:, r * rows_in : (r + 1) * rows_in], value)
        g_class[...] = value

    return pl.pallas_call(
        kernel,
        name="finish",
        out_shape=[
            jax.ShapeDtypeStruct((dpc, patch), F32),
            jax.ShapeDtypeStruct((tok, dpc), F32),
            jax.ShapeDtypeStruct((cin, d), F32),
            jax.ShapeDtypeStruct((dpc, ff), F32),
            jax.ShapeDtypeStruct((classes, rows_in), F32),
        ],
        compiler_params=pltpu.CompilerParams(vmem_limit_bytes=32 * 1024 * 1024),
    )


def swap_bit(block, bit):
    count = lax.axis_size("client")
    return lax.ppermute(block, "client", [(i, i ^ (1 << bit)) for i in range(count)])


def swap_by_core(block, even, odd):
    count = lax.axis_size("client")
    return lax.ppermute(
        block, "client", [(i, i ^ (1 << (even if i % 2 == 0 else odd))) for i in range(count)]
    )


def per_device(
    patches,
    labels,
    assign,
    patch_embed,
    positions,
    client_in,
    client_down,
    server_in,
    server_down,
    classifier,
):
    members = lax.axis_size("client")
    group = members // SHARDS
    group_bits = group.bit_length() - 1
    bits = members.bit_length() - 1
    patch, d = patch_embed.shape
    tok = positions.shape[0]
    ff = client_down.shape[0]
    img = labels.shape[0] // members
    layers = server_in.shape[0] + 1
    pr = patches.shape[0] // group
    cin = client_in.shape[1] // members
    capacity = SLOTS * group

    pieces, first = [1], [0]
    piece_in, piece_down = [server_in[None]], [server_down[None]]
    for bit in range(group_bits):
        whole_in = piece_in[0] if bit == 0 else jnp.concatenate(piece_in, 0)
        whole_down = piece_down[0] if bit == 0 else jnp.concatenate(piece_down, 0)
        piece_in.append(swap_bit(whole_in, bit))
        piece_down.append(swap_bit(whole_down, bit))
        first.append(1 << bit)
        pieces.append(1 << bit)

    cfg = dict(
        d=d,
        ff=ff,
        tok=tok,
        patch=patch,
        members=members,
        group=group,
        capacity=capacity,
        pr=pr,
        images=capacity * pr // tok,
        classes=classifier.shape[2],
        layers=layers,
        bits=bits,
        cin=cin,
        cin_pad=-(-cin // ROWS16) * ROWS16,
        heights=[-(-cin // ROWS16) * ROWS16 + ROWS16, (ff // d - 1) * ROWS16],
        vmem=(47 if bits <= 5 else 58) * 2**20,
        pieces=pieces,
        first=first,
        packed=patch // group,
        img=img,
    )
    others = piece_in[1:] + piece_down[1:]
    others = make_stage([array.shape for array in others])(*others)
    piece_in[1:], piece_down[1:] = others[:group_bits], others[group_bits:]

    outgoing = make_pack(cfg)(patches.T)
    arrived = lax.all_to_all(outgoing, "client", split_axis=0, concat_axis=0, tiled=True)
    results = make_chain(cfg)(
        assign.reshape(-1),
        labels,
        arrived,
        *[
            pltpu.with_memory_space_constraint(array, pltpu.HBM)
            for array in (
                patch_embed,
                positions,
                client_in,
                client_down,
                *piece_in,
                *piece_down,
                classifier.transpose(2, 0, 1),
            )
        ],
    )
    losses, dcls = results[:2]
    grads = results[2 : 2 + 2 * PIECES]
    saved = results[2 + 2 * PIECES :]

    keeps, sends = list(grads[0::2]), list(grads[1::2])
    for bit in range(group_bits):
        dcls = dcls + swap_bit(dcls, bit)
    recvs = [swap_bit(send, 0) for send in sends]
    for step in range(bits - 1):
        for piece in range(PIECES):
            keep, recv = keeps[piece], recvs[piece]
            half = keep.shape[0] // 2
            sends[piece] = (keep[half:].astype(F32) + recv[half:].astype(F32)).astype(BF)
            keeps[piece] = (keep[:half].astype(F32) + recv[:half].astype(F32)).astype(BF)
        if step == 0:
            sends, saved, dcls = lax.optimization_barrier((sends, saved, dcls))
        if step == bits - 2:
            parts = make_server_grads(cfg)(*[pltpu.with_memory_space_constraint(array, pltpu.HBM) for array in saved])
            keep_in, send_in, keep_down, send_down = parts
            for bit in range(group_bits - 1, -1, -1):
                recv_in, recv_down = swap_bit(send_in, bit), swap_bit(send_down, bit)
                if bit == 0:
                    sends, keep_in, keep_down = lax.optimization_barrier((sends, keep_in, keep_down))
                got_in = keep_in.astype(F32) + recv_in.astype(F32)
                got_down = keep_down.astype(F32) + recv_down.astype(F32)
                half = got_in.shape[0] // 2
                keep_in, send_in = got_in[:half], got_in[half:].astype(BF)
                keep_down, send_down = got_down[:half], got_down[half:].astype(BF)
        if step == bits - 2:
            recvs = swap_bit(jnp.concatenate(sends, axis=1), bits - 1)
            continue
        for piece in range(PIECES):
            even, odd = [order[step] for order in stage_orders(bits, piece)]
            recvs[piece] = swap_by_core(sends[piece], even, odd)
    recvs, got_in, got_down = lax.optimization_barrier((recvs, got_in, got_down))
    g_embed, g_pos, g_client_in, g_client_down, g_class = make_finish(cfg)(*keeps, recvs, dcls)

    return (
        losses,
        g_embed.T,
        g_pos,
        g_client_in.T,
        g_client_down.T,
        got_in[0],
        got_down[0],
        g_class.T,
    )


def solution(mesh):
    in_specs = (
        P("client", None),
        P(),
        P(),
        P(),
        P(),
        P(),
        P(),
        P(None, "client", None),
        P(None, "client", None),
        P(),
    )
    out_specs = (
        P("client", None),
        P(None, "client"),
        P(None, "client"),
        P(None, "client"),
        P(None, "client"),
        P(None, "client", None),
        P(None, "client", None),
        P("client", None),
    )
    return jax.shard_map(
        per_device, mesh=mesh, in_specs=in_specs, out_specs=out_specs, check_vma=False
    )
```

profile of v0, /device:TPU:0, one launch (start us, length us, event | category | flops | bytes accessed | tf_op | source)
XLA Modules:
  0.0 193.4 jit_solution(7757594426353652901)
XLA Ops:
  0.6 0.6 collective-permute-start
  1.2 1.8 pack.1
  3.0 6.9 %all-to-all-start = ((bf16[32,96,128]{2,1,0:T(8,128)(2,1)}), bf16[32,96,128]{2,1,0:T(8,128)(2,1)S(1)}, u32[]{:S(2)}, u32[]{:S(2)}) async-start(bf16[32,96,128]{2,1,0:T(8,128)(2,1)} %pack.1), calls=%async_computation | async-start | bytes 1572864 | tf_op jit(solution)/shard_map/all_to_all | solution.py:727
  10.0 0.3 collective-permute-start.1
  10.3 2.9 %collective-permute-done.1.refs_1_ = bf16[1,2,768,384]{3,2,1,0:T(8,128)(2,1)} collective-permute-done((bf16[1,2,768,384]{3,2,1,0:T(8,128)(2,1)}, bf16[1,2,768,384]{3,2,1,0:T(8,128)(2,1)}, u32[]{:S(2)}, u32[]{:S(2)}) %collective-permute-start.1) | collective-permute-done | bytes 1179680 | tf_op jit(solution)/shard_map/ppermute | solution.py:655
  13.3 1.4 copy-done.2
  14.7 108.3 %stage.1 = (bf16[1,2,192,3072]{3,2,1,0:T(8,128)(2,1)}, bf16[1,2,768,384]{3,2,1,0:T(8,128)(2,1)}) custom-call(bf16[1,2,192,3072]{3,2,1,0:T(8,128)(2,1)} %copy-done.2, bf16[1,2,768,384]{3,2,1,0:T(8,128)(2,1)} %collective-permute-done.1.refs_1_), custom_call_target="tpu_custom_call" | custom-call | tf_op jit(solution)/shard_map/stage/pallas_call | solution.py:723
  123.0 23.9 %chain.1 = (f32[1,16]{1,0:T(1,128)}, f32[10,384]{1,0:T(8,128)S(1)}, bf16[16,112,384]{2,1,0:T(8,128)(2,1)S(1)}, bf16[16,112,384]{2,1,0:T(8,128)(2,1)S(1)}, bf16[1...) custom-call(s32[32]{0:T(128)S(1)} %bitcast.11, ...), custom_call_target="tpu_custom_call" | custom-call | tf_op jit(solution)/shard_map/chain/pallas_call | solution.py:728
  146.9 0.3 collective-permute-start.2
  147.2 0.3 collective-permute-start.3
  147.5 0.2 collective-permute-start.4
  147.7 3.3 %collective-permute-done.4 = f32[10,384]{1,0:T(8,128)S(1)} collective-permute-done((f32[10,384]{1,0:T(8,128)S(1)}, f32[10,384]{1,0:T(8,128)S(1)}, u32[]{:S(2)}, u32[]{:S(2)}) %collective-permute-start.4) | collective-permute-done | bytes 15392 | tf_op jit(solution)/shard_map/ppermute | solution.py:655
  151.0 0.2 add_convert_fusion.4
  151.2 0.4 add_convert_fusion.1
  151.6 1.8 collective-permute-start.5
  153.4 6.5 %server_grads.1 = (bf16[1,2,192,3072]{3,2,1,0:T(8,128)(2,1)S(1)}, bf16[1,2,192,3072]{3,2,1,0:T(8,128)(2,1)S(1)}, bf16[1,2,768,384]{3,2,1,0:T(8,128)(2,1)S(1)}, bf16[1,2,768,384]{3,2,1,0:T(8,128)(2,1)S(1)}) custom-call(bf16[2,256,384]{2,1,0:T(8,128)(2,1)} %get-tuple-element.69.refs_0_, bf16[2,256,384]{2,1,0:T(8,128)(2,1)} %get-tuple-element.70.refs_1_, ...), custom_call_target="tpu_custom_call" | custom-call | flops 3623878656 | bytes 16777216 | tf_op jit(solution)/shard_map/server_grads/pallas_call | solution.py:762
  160.0 1.5 collective-permute-start.8
  161.5 0.2 collective-permute-start.13
  161.6 7.7 %collective-permute-done.8 = bf16[8,48,384]{2,1,0:T(8,128)(2,1)S(1)} collective-permute-done((bf16[8,48,384]{2,1,0:T(8,128)(2,1)S(1)}, bf16[8,48,384]{2,1,0:T(8,128)(2,1)S(1)}, u32[]{:S(2)}, u32[]{:S(2)}) %collective-permute-start.8) | collective-permute-done | bytes 294944 | tf_op jit(solution)/shard_map/ppermute | solution.py:660
  169.4 0.9 collective-permute-start.9
  170.4 0.2 add_convert_fusion.3
  170.6 1.2 collective-permute-start.6
  171.7 3.1 %collective-permute-done.9 = bf16[4,48,384]{2,1,0:T(8,128)(2,1)S(1)} collective-permute-done((bf16[4,48,384]{2,1,0:T(8,128)(2,1)S(1)}, bf16[4,48,384]{2,1,0:T(8,128)(2,1)S(1)}, u32[]{:S(2)}, u32[]{:S(2)}) %collective-permute-start.9) | collective-permute-done | bytes 147488 | tf_op jit(solution)/shard_map/ppermute | solution.py:660
  174.9 1.5 collective-permute-start.10
  176.4 2.3 %collective-permute-done.6 = bf16[4,112,384]{2,1,0:T(8,128)(2,1)S(1)} collective-permute-done((bf16[4,112,384]{2,1,0:T(8,128)(2,1)S(1)}, bf16[4,112,384]{2,1,0:T(8,128)(2,1)S(1)}, u32[]{:S(2)}, u32[]{:S(2)}) %collective-permute-start.6) | collective-permute-done | bytes 344096 | tf_op jit(solution)/shard_map/ppermute | solution.py:660
  178.7 0.1 add_convert_fusion.7
  178.8 1.5 collective-permute-start.7
  180.3 5.0 %collective-permute-done.7 = bf16[2,112,384]{2,1,0:T(8,128)(2,1)S(1)} collective-permute-done((bf16[2,112,384]{2,1,0:T(8,128)(2,1)S(1)}, bf16[2,112,384]{2,1,0:T(8,128)(2,1)S(1)}, u32[]{:S(2)}, u32[]{:S(2)}) %collective-permute-start.7) | collective-permute-done | bytes 172064 | tf_op jit(solution)/shard_map/ppermute | solution.py:660
  185.4 2.4 %collective-permute-start.11 = (bf16[1,160,384]{2,1,0:T(8,128)(2,1)S(1)}, bf16[1,160,384]{2,1,0:T(8,128)(2,1)S(1)}, u32[]{:S(2)}, u32[]{:S(2)}) collective-permute-start(bf16[1,160,384]{2,1,0:T(8,128)(2,1)S(1)} %pad_maximum_fusion), channel_id=1, source_target_pairs={{0,16},{1,17},{2,18},{3,19},{4,20},{5,21},{6,22},{7,23},{8,24},{9,... | collective-permute-start | bytes 368648 | tf_op jit(solution)/shard_map/ppermute | solution.py:655
  187.9 1.6 convert_add_fusion.1
  189.5 3.0 %convert_add_fusion = f32[1,2,192,3072]{3,2,1,0:T(8,128)} fusion(bf16[1,2,192,3072]{3,2,1,0:T(8,128)(2,1)S(1)} %collective-permute-done.12, bf16[1,2,192,3072]{3,2,1,0:T(8,128)(2,1)S(1)} %get-tuple-element.81), kind=kLoop, calls=%fused_computation | loop fusion | flops 3538944 | bytes 9437184 | tf_op jit(solution)/shard_map/add | solution.py:768
  192.6 0.8 finish.1
  (21 shorter events, 0.3 us)
Async XLA Ops:
  0.6 12.6 %collective-permute-start = (bf16[1,2,192,3072]{3,2,1,0:T(8,128)(2,1)}, bf16[1,2,192,3072]{3,2,1,0:T(8,128)(2,1)S(1)}, u32[]{:S(2)}, u32[]{:S(2)}) collective-permute-start(bf16[1,2,192,3072]{3,2,1,0:T(8,128)(2,1)} %bitcast.14), channel_id=1, source_target_pairs={{0,1},{1,0},{2,3},{3,2},{4,5},{5,4},{6,7},{7,6},{8,9},{9,8},{10,11... | collective-permute-start | bytes 7077896 | tf_op jit(solution)/shard_map/ppermute | solution.py:655
  3.0 120.0 %all-to-all-start = ((bf16[32,96,128]{2,1,0:T(8,128)(2,1)}), bf16[32,96,128]{2,1,0:T(8,128)(2,1)S(1)}, u32[]{:S(2)}, u32[]{:S(2)}) async-start(bf16[32,96,128]{2,1,0:T(8,128)(2,1)} %pack.1), calls=%async_computation | async-start | bytes 1572864 | tf_op jit(solution)/shard_map/all_to_all | solution.py:727
  10.0 113.0 %copy-start = (s32[256]{0:T(256)S(1)}, s32[256]{0:T(256)}, u32[]{:S(2)}) copy-start(s32[256]{0:T(256)} %refs_1_.1) | copy-start | bytes 3076
  10.0 113.0 %copy-start.1 = (s32[32,1]{0,1:T(1,128)S(1)}, s32[32,1]{0,1:T(1,128)}, u32[]{:S(2)}) copy-start(s32[32,1]{0,1:T(1,128)} %param.12) | copy-start | bytes 388
  10.0 3.3 %collective-permute-start.1 = (bf16[1,2,768,384]{3,2,1,0:T(8,128)(2,1)}, bf16[1,2,768,384]{3,2,1,0:T(8,128)(2,1)}, u32[]{:S(2)}, u32[]{:S(2)}) collective-permute-start(bf16[1,2,768,384]{3,2,1,0:T(8,128)(2,1)} %bitcast.16), channel_id=1, source_target_pairs={{0,1},{1,0},{2,3},{3,2},{4,5},{5,4},{6,7},{7,6},{8,9},{9,8},{10,11... | collective-permute-start | bytes 3538952 | tf_op jit(solution)/shard_map/ppermute | solution.py:655
  13.3 1.4 copy-start.2
  146.9 4.2 %collective-permute-start.2 = (bf16[16,112,384]{2,1,0:T(8,128)(2,1)S(1)}, bf16[16,112,384]{2,1,0:T(8,128)(2,1)S(1)}, u32[]{:S(2)}, u32[]{:S(2)}) collective-permute-start(bf16[16,112,384]{2,1,0:T(8,128)(2,1)S(1)} %get-tuple-element.55), channel_id=1, source_target_pairs={{0,1},{1,0},{2,3},{3,2},{4,5},{5,4},{6,7},{7,6},{8,9},{9,8},{10,11... | collective-permute-start | bytes 4128776 | tf_op jit(solution)/shard_map/ppermute | solution.py:655
  147.2 3.8 %collective-permute-start.3 = (bf16[16,48,384]{2,1,0:T(8,128)(2,1)S(1)}, bf16[16,48,384]{2,1,0:T(8,128)(2,1)S(1)}, u32[]{:S(2)}, u32[]{:S(2)}) collective-permute-start(bf16[16,48,384]{2,1,0:T(8,128)(2,1)S(1)} %get-tuple-element.57), channel_id=1, source_target_pairs={{0,1},{1,0},{2,3},{3,2},{4,5},{5,4},{6,7},{7,6},{8,9},{9,8},{10,11... | collective-permute-start | bytes 1769480 | tf_op jit(solution)/shard_map/ppermute | solution.py:655
  147.5 3.5 %collective-permute-start.4 = (f32[10,384]{1,0:T(8,128)S(1)}, f32[10,384]{1,0:T(8,128)S(1)}, u32[]{:S(2)}, u32[]{:S(2)}) collective-permute-start(f32[10,384]{1,0:T(8,128)S(1)} %get-tuple-element.66), channel_id=1, source_target_pairs={{0,1},{1,0},{2,3},{3,2},{4,5},{5,4},{6,7},{7,6},{8,9},{9,8},{10,11... | collective-permute-start | bytes 46088 | tf_op jit(solution)/shard_map/ppermute | solution.py:655
  151.6 18.8 %collective-permute-start.5 = (bf16[8,112,384]{2,1,0:T(8,128)(2,1)S(1)}, bf16[8,112,384]{2,1,0:T(8,128)(2,1)S(1)}, u32[]{:S(2)}, u32[]{:S(2)}) collective-permute-start(bf16[8,112,384]{2,1,0:T(8,128)(2,1)S(1)} %get-tuple-element.67), channel_id=1, source_target_pairs={{0,2},{1,5},{2,0},{3,7},{4,6},{5,1},{6,4},{7,3},{8,10},{9,13},{10,... | collective-permute-start | bytes 2064392 | tf_op jit(solution)/shard_map/ppermute | solution.py:660
  159.9 29.6 %collective-permute-start.12 = (bf16[1,2,192,3072]{3,2,1,0:T(8,128)(2,1)S(1)}, bf16[1,2,192,3072]{3,2,1,0:T(8,128)(2,1)S(1)}, u32[]{:S(2)}, u32[]{:S(2)}) collective-permute-start(bf16[1,2,192,3072]{3,2,1,0:T(8,128)(2,1)S(1)} %get-tuple-element.82), channel_id=1, source_target_pairs={{0,1},{1,0},{2,3},{3,2},{4,5},{5,4},{6,7},{7,6},{8,9},{9,8},{10,11... | collective-permute-start | bytes 7077896 | tf_op jit(solution)/shard_map/ppermute | solution.py:655
  160.0 9.4 %collective-permute-start.8 = (bf16[8,48,384]{2,1,0:T(8,128)(2,1)S(1)}, bf16[8,48,384]{2,1,0:T(8,128)(2,1)S(1)}, u32[]{:S(2)}, u32[]{:S(2)}) collective-permute-start(bf16[8,48,384]{2,1,0:T(8,128)(2,1)S(1)} %get-tuple-element.68), channel_id=1, source_target_pairs={{0,8},{1,9},{2,10},{3,11},{4,12},{5,13},{6,14},{7,15},{8,0},{9,1},... | collective-permute-start | bytes 884744 | tf_op jit(solution)/shard_map/ppermute | solution.py:660
  161.5 26.4 %collective-permute-start.13 = (bf16[1,2,768,384]{3,2,1,0:T(8,128)(2,1)S(1)}, bf16[1,2,768,384]{3,2,1,0:T(8,128)(2,1)S(1)}, u32[]{:S(2)}, u32[]{:S(2)}) collective-permute-start(bf16[1,2,768,384]{3,2,1,0:T(8,128)(2,1)S(1)} %get-tuple-element.84), channel_id=1, source_target_pairs={{0,1},{1,0},{2,3},{3,2},{4,5},{5,4},{6,7},{7,6},{8,9},{9,8},{10,11... | collective-permute-start | bytes 3538952 | tf_op jit(solution)/shard_map/ppermute | solution.py:655
  169.4 5.4 %collective-permute-start.9 = (bf16[4,48,384]{2,1,0:T(8,128)(2,1)S(1)}, bf16[4,48,384]{2,1,0:T(8,128)(2,1)S(1)}, u32[]{:S(2)}, u32[]{:S(2)}) collective-permute-start(bf16[4,48,384]{2,1,0:T(8,128)(2,1)S(1)} %get-tuple-element.103), channel_id=1, source_target_pairs={{0,2},{1,3},{2,0},{3,1},{4,6},{5,7},{6,4},{7,5},{8,10},{9,11},{10,... | collective-permute-start | bytes 442376 | tf_op jit(solution)/shard_map/ppermute | solution.py:660
  170.6 8.1 %collective-permute-start.6 = (bf16[4,112,384]{2,1,0:T(8,128)(2,1)S(1)}, bf16[4,112,384]{2,1,0:T(8,128)(2,1)S(1)}, u32[]{:S(2)}, u32[]{:S(2)}) collective-permute-start(bf16[4,112,384]{2,1,0:T(8,128)(2,1)S(1)} %get-tuple-element.97), channel_id=1, source_target_pairs={{0,4},{1,9},{2,6},{3,11},{4,0},{5,13},{6,2},{7,15},{8,12},{9,1},{1... | collective-permute-start | bytes 1032200 | tf_op jit(solution)/shard_map/ppermute | solution.py:660
  174.9 5.4 %collective-permute-start.10 = (bf16[2,48,384]{2,1,0:T(8,128)(2,1)S(1)}, bf16[2,48,384]{2,1,0:T(8,128)(2,1)S(1)}, u32[]{:S(2)}, u32[]{:S(2)}) collective-permute-start(bf16[2,48,384]{2,1,0:T(8,128)(2,1)S(1)} %get-tuple-element.107), channel_id=1, source_target_pairs={{0,4},{1,5},{2,6},{3,7},{4,0},{5,1},{6,2},{7,3},{8,12},{9,13},{10,... | collective-permute-start | bytes 221192 | tf_op jit(solution)/shard_map/ppermute | solution.py:660
  178.8 6.6 %collective-permute-start.7 = (bf16[2,112,384]{2,1,0:T(8,128)(2,1)S(1)}, bf16[2,112,384]{2,1,0:T(8,128)(2,1)S(1)}, u32[]{:S(2)}, u32[]{:S(2)}) collective-permute-start(bf16[2,112,384]{2,1,0:T(8,128)(2,1)S(1)} %get-tuple-element.101), channel_id=1, source_target_pairs={{0,8},{1,3},{2,10},{3,1},{4,12},{5,7},{6,14},{7,5},{8,0},{9,11},{1... | collective-permute-start | bytes 516104 | tf_op jit(solution)/shard_map/ppermute | solution.py:660
  185.4 7.2 %collective-permute-start.11 = (bf16[1,160,384]{2,1,0:T(8,128)(2,1)S(1)}, bf16[1,160,384]{2,1,0:T(8,128)(2,1)S(1)}, u32[]{:S(2)}, u32[]{:S(2)}) collective-permute-start(bf16[1,160,384]{2,1,0:T(8,128)(2,1)S(1)} %pad_maximum_fusion), channel_id=1, source_target_pairs={{0,16},{1,17},{2,18},{3,19},{4,20},{5,21},{6,22},{7,23},{8,24},{9,... | collective-permute-start | bytes 368648 | tf_op jit(solution)/shard_map/ppermute | solution.py:655
where the time goes:
time: 194 us; the launch traced here: 193 us
  Pallas kernels  141 us (73%)
  waiting for transfers between devices  24.5 us (13%)
  starting transfers between devices  19.7 us (10%)
  other arithmetic  5.67 us (3%)
    pallas_call x1, Pallas kernels, per_device(): others = make_stage([array.shape for array in others])(*others)  108 us
    pallas_call x1, Pallas kernels, per_device(): make_chain(cfg)  23.9 us
    ppermute x6, waiting for transfers between devices, swap_by_core(): lax.ppermute(block, 'client', [(i, i ^ 1 << (even if i % 2 == 0 else odd)...  18.2 us
    ppermute x6, starting transfers between devices, swap_by_core(): lax.ppermute(block, 'client', [(i, i ^ 1 << (even if i % 2 == 0 else odd)...  8.48 us
    all_to_all x1, starting transfers between devices, per_device(): lax.all_to_all(outgoing, 'client', split_axis=0, concat_axis=0, tiled=True)  6.95 us
    pallas_call x1, Pallas kernels, per_device(): make_server_grads(cfg)  6.48 us
    ppermute x8, waiting for transfers between devices, swap_bit(): lax.ppermute(block, 'client', [(i, i ^ 1 << bit) for i in range(count)])  6.26 us
    ppermute x8, starting transfers between devices, swap_bit(): lax.ppermute(block, 'client', [(i, i ^ 1 << bit) for i in range(count)])  4.33 us
  transfers between devices with their start and end apart: 15, of which 6 were waited for; matrix products, arithmetic and copies ran while one was open for 3% of the time, Pallas kernels for 60%

commit v1 on v0

--- a/solution.py
+++ b/solution.py
@@ -498,11 +498,15 @@
     count = len(shapes)
 
     def kernel(*refs):
-        sources, targets, sems = refs[:count], refs[count : 2 * count], refs[2 * count]
-        copies = [pltpu.make_async_copy(sources[i], targets[i], sems.at[i]) for i in range(count)]
-        for copy in copies:
+        sources, targets, local, sems = refs[:count], refs[count : 2 * count], refs[2 * count : -1], refs[-1]
+        loads = [pltpu.make_async_copy(sources[i], local[i], sems.at[i]) for i in range(count)]
+        stores = [pltpu.make_async_copy(local[i], targets[i], sems.at[count + i]) for i in range(count)]
+        for copy in loads:
             copy.start()
-        for copy in copies:
+        for load, store in zip(loads, stores):
+            load.wait()
+            store.start()
+        for copy in stores:
             copy.wait()
 
     return pl.pallas_call(
@@ -511,7 +515,8 @@
         in_specs=[pl.BlockSpec(memory_space=pl.ANY)] * count,
         out_specs=[pl.BlockSpec(memory_space=pltpu.HBM)] * count,
         out_shape=[pltpu.HBM(shape, BF) for shape in shapes],
-        scratch_shapes=[pltpu.SemaphoreType.DMA((count,))],
+        scratch_shapes=[pltpu.VMEM(shape, BF) for shape in shapes] + [pltpu.SemaphoreType.DMA((2 * count,))],
+        compiler_params=pltpu.CompilerParams(vmem_limit_bytes=16 * 2**20),
     )
 
 

time: 194 us -> 101 us (0.52)
  Pallas kernels: 141 us -> 35.2 us
  waiting for transfers between devices: 24.5 us -> 42.8 us
  starting transfers between devices: 19.7 us -> 16.1 us
    pallas_call x1, Pallas kernels: 108 us -> 2.24 us  [per_device(): others = make_stage([array.shape for array in others])(*others)]
    all_to_all x1, waiting for transfers between devices: 0.01 us -> 15.2 us  [per_device(): lax.all_to_all(outgoing, 'client', split_axis=0, concat_axis=0, tiled=True)]
    ppermute x8, starting transfers between devices: 4.33 us -> 1.81 us  [swap_bit(): lax.ppermute(block, 'client', [(i, i ^ 1 << bit) for i in range(count)])]
    ppermute x8, waiting for transfers between devices: 6.26 us -> 8.62 us  [swap_bit(): lax.ppermute(block, 'client', [(i, i ^ 1 << bit) for i in range(count)])]
  transfers between devices with their start and end apart: 15 -> 15, of which waited for: 6 -> 8; matrix products, arithmetic and copies ran while one was open for 3% -> 5% of each run, Pallas kernels for 60% -> 10%
where the time goes in v1:
time: 101 us
  waiting for transfers between devices  42.8 us (42%)
  Pallas kernels  35.2 us (35%)
  starting transfers between devices  16.1 us (16%)
  other arithmetic  5.67 us (6%)
    pallas_call x1, Pallas kernels, per_device(): make_chain(cfg)  23.8 us
    ppermute x6, waiting for transfers between devices, swap_by_core(): lax.ppermute(block, 'client', [(i, i ^ 1 << (even if i % 2 == 0 else odd)...  19 us
    all_to_all x1, waiting for transfers between devices, per_device(): lax.all_to_all(outgoing, 'client', split_axis=0, concat_axis=0, tiled=True)  15.2 us
    ppermute x8, waiting for transfers between devices, swap_bit(): lax.ppermute(block, 'client', [(i, i ^ 1 << bit) for i in range(count)])  8.62 us
    ppermute x6, starting transfers between devices, swap_by_core(): lax.ppermute(block, 'client', [(i, i ^ 1 << (even if i % 2 == 0 else odd)...  7.31 us
    all_to_all x1, starting transfers between devices, per_device(): lax.all_to_all(outgoing, 'client', split_axis=0, concat_axis=0, tiled=True)  6.95 us
    pallas_call x1, Pallas kernels, per_device(): make_server_grads(cfg)  6.48 us
    add x1, other arithmetic, per_device(): got_in = keep_in.astype(F32) + recv_in.astype(F32)  3.04 us
  transfers between devices with their start and end apart: 15, of which 8 were waited for; matrix products, arithmetic and copies ran while one was open for 5% of the time, Pallas kernels for 10%

profile of v1, /device:TPU:0, one launch (start us, length us, event | category | flops | bytes accessed | tf_op | source)
XLA Modules:
  0.0 100.5 jit_solution(11338511102022013066)
XLA Ops:
  0.6 0.6 collective-permute-start
  1.2 1.8 %pack.1 = bf16[32,96,128]{2,1,0:T(8,128)(2,1)} custom-call(bf16[192,128]{1,0:T(8,128)(2,1)} %bitcast.19), custom_call_target="tpu_custom_call" | custom-call | tf_op jit(solution)/shard_map/pack/pallas_call | solution.py:731
  3.0 6.9 %all-to-all-start = ((bf16[32,96,128]{2,1,0:T(8,128)(2,1)}), bf16[32,96,128]{2,1,0:T(8,128)(2,1)S(1)}, u32[]{:S(2)}, u32[]{:S(2)}) async-start(bf16[32,96,128]{2,1,0:T(8,128)(2,1)} %pack.1), calls=%async_computation | async-start | bytes 1572864 | tf_op jit(solution)/shard_map/all_to_all | solution.py:732
  10.0 0.3 collective-permute-start.1
  10.3 2.8 %collective-permute-done.1.refs_1_ = bf16[1,2,768,384]{3,2,1,0:T(8,128)(2,1)S(1)} collective-permute-done((bf16[1,2,768,384]{3,2,1,0:T(8,128)(2,1)}, bf16[1,2,768,384]{3,2,1,0:T(8,128)(2,1)S(1)}, u32[]{:S(2)}, u32[]{:S(2)}) %collective-permute-start.1) | collective-permute-done | bytes 1179680 | tf_op jit(solution)/shard_map/ppermute | solution.py:660
  13.1 2.2 %stage.1 = (bf16[1,2,192,3072]{3,2,1,0:T(8,128)(2,1)}, bf16[1,2,768,384]{3,2,1,0:T(8,128)(2,1)}) custom-call(bf16[1,2,192,3072]{3,2,1,0:T(8,128)(2,1)S(1)} %collective-permute-done.refs_0_, bf16[1,2,768,384]{3,2,1,0:T(8,128)(2,1)S(1)} %collective-permute-done.1.refs_1_), custom_call_target="tpu_custom_call" | custom-call | tf_op jit(solution)/shard_map/stage/pallas_call | solution.py:728
  15.4 15.2 %all-to-all-done.refs_2_ = bf16[32,96,128]{2,1,0:T(8,128)(2,1)S(1)} async-done(((bf16[32,96,128]{2,1,0:T(8,128)(2,1)}), bf16[32,96,128]{2,1,0:T(8,128)(2,1)S(1)}, u32[]{:S(2)}, u32[]{:S(2)}) %all-to-all-start) | async-done | bytes 786464 | tf_op jit(solution)/shard_map/all_to_all | solution.py:732
  30.6 23.8 %chain.1 = (f32[1,16]{1,0:T(1,128)}, f32[10,384]{1,0:T(8,128)S(1)}, bf16[16,112,384]{2,1,0:T(8,128)(2,1)S(1)}, bf16[16,112,384]{2,1,0:T(8,128)(2,1)S(1)}, bf16[1...) custom-call(s32[32]{0:T(128)S(1)} %bitcast.11, ...), custom_call_target="tpu_custom_call" | custom-call | tf_op jit(solution)/shard_map/chain/pallas_call | solution.py:733
  54.5 0.5 collective-permute-start.3
  55.0 0.1 collective-permute-start.4
  55.1 3.4 %collective-permute-done.4 = f32[10,384]{1,0:T(8,128)S(1)} collective-permute-done((f32[10,384]{1,0:T(8,128)S(1)}, f32[10,384]{1,0:T(8,128)S(1)}, u32[]{:S(2)}, u32[]{:S(2)}) %collective-permute-start.4) | collective-permute-done | bytes 15392 | tf_op jit(solution)/shard_map/ppermute | solution.py:660
  58.5 0.2 add_convert_fusion.4
  58.7 0.4 add_convert_fusion.1
  59.0 1.5 %collective-permute-start.5 = (bf16[8,112,384]{2,1,0:T(8,128)(2,1)S(1)}, bf16[8,112,384]{2,1,0:T(8,128)(2,1)S(1)}, u32[]{:S(2)}, u32[]{:S(2)}) collective-permute-start(bf16[8,112,384]{2,1,0:T(8,128)(2,1)S(1)} %get-tuple-element.67), channel_id=1, source_target_pairs={{0,2},{1,5},{2,0},{3,7},{4,6},{5,1},{6,4},{7,3},{8,10},{9,13},{10,... | collective-permute-start | bytes 2064392 | tf_op jit(solution)/shard_map/ppermute | solution.py:665
  60.6 6.5 %server_grads.1 = (bf16[1,2,192,3072]{3,2,1,0:T(8,128)(2,1)S(1)}, bf16[1,2,192,3072]{3,2,1,0:T(8,128)(2,1)S(1)}, bf16[1,2,768,384]{3,2,1,0:T(8,128)(2,1)S(1)}, bf16[1,2,768,384]{3,2,1,0:T(8,128)(2,1)S(1)}) custom-call(bf16[2,256,384]{2,1,0:T(8,128)(2,1)} %get-tuple-element.69.refs_0_, bf16[2,256,384]{2,1,0:T(8,128)(2,1)} %get-tuple-element.70.refs_1_, ...), custom_call_target="tpu_custom_call" | custom-call | flops 3623878656 | bytes 16777216 | tf_op jit(solution)/shard_map/server_grads/pallas_call | solution.py:767
  67.1 0.8 collective-permute-start.8
  67.9 0.1 collective-permute-start.13
  68.1 8.5 %collective-permute-done.8 = bf16[8,48,384]{2,1,0:T(8,128)(2,1)S(1)} collective-permute-done((bf16[8,48,384]{2,1,0:T(8,128)(2,1)S(1)}, bf16[8,48,384]{2,1,0:T(8,128)(2,1)S(1)}, u32[]{:S(2)}, u32[]{:S(2)}) %collective-permute-start.8) | collective-permute-done | bytes 294944 | tf_op jit(solution)/shard_map/ppermute | solution.py:665
  76.5 0.1 add_convert_fusion.9
  76.6 1.0 collective-permute-start.9
  77.6 0.2 add_convert_fusion.3
  77.8 1.3 %collective-permute-start.6 = (bf16[4,112,384]{2,1,0:T(8,128)(2,1)S(1)}, bf16[4,112,384]{2,1,0:T(8,128)(2,1)S(1)}, u32[]{:S(2)}, u32[]{:S(2)}) collective-permute-start(bf16[4,112,384]{2,1,0:T(8,128)(2,1)S(1)} %get-tuple-element.97), channel_id=1, source_target_pairs={{0,4},{1,9},{2,6},{3,11},{4,0},{5,13},{6,2},{7,15},{8,12},{9,1},{1... | collective-permute-start | bytes 1032200 | tf_op jit(solution)/shard_map/ppermute | solution.py:665
  79.1 2.9 %collective-permute-done.9 = bf16[4,48,384]{2,1,0:T(8,128)(2,1)S(1)} collective-permute-done((bf16[4,48,384]{2,1,0:T(8,128)(2,1)S(1)}, bf16[4,48,384]{2,1,0:T(8,128)(2,1)S(1)}, u32[]{:S(2)}, u32[]{:S(2)}) %collective-permute-start.9) | collective-permute-done | bytes 147488 | tf_op jit(solution)/shard_map/ppermute | solution.py:665
  82.1 1.6 %collective-permute-start.10 = (bf16[2,48,384]{2,1,0:T(8,128)(2,1)S(1)}, bf16[2,48,384]{2,1,0:T(8,128)(2,1)S(1)}, u32[]{:S(2)}, u32[]{:S(2)}) collective-permute-start(bf16[2,48,384]{2,1,0:T(8,128)(2,1)S(1)} %get-tuple-element.107), channel_id=1, source_target_pairs={{0,4},{1,5},{2,6},{3,7},{4,0},{5,1},{6,2},{7,3},{8,12},{9,13},{10,... | collective-permute-start | bytes 221192 | tf_op jit(solution)/shard_map/ppermute | solution.py:665
  83.6 2.3 %collective-permute-done.6 = bf16[4,112,384]{2,1,0:T(8,128)(2,1)S(1)} collective-permute-done((bf16[4,112,384]{2,1,0:T(8,128)(2,1)S(1)}, bf16[4,112,384]{2,1,0:T(8,128)(2,1)S(1)}, u32[]{:S(2)}, u32[]{:S(2)}) %collective-permute-start.6) | collective-permute-done | bytes 344096 | tf_op jit(solution)/shard_map/ppermute | solution.py:665
  85.9 0.1 add_convert_fusion.7
  86.0 1.2 %collective-permute-start.7 = (bf16[2,112,384]{2,1,0:T(8,128)(2,1)S(1)}, bf16[2,112,384]{2,1,0:T(8,128)(2,1)S(1)}, u32[]{:S(2)}, u32[]{:S(2)}) collective-permute-start(bf16[2,112,384]{2,1,0:T(8,128)(2,1)S(1)} %get-tuple-element.101), channel_id=1, source_target_pairs={{0,8},{1,3},{2,10},{3,1},{4,12},{5,7},{6,14},{7,5},{8,0},{9,11},{1... | collective-permute-start | bytes 516104 | tf_op jit(solution)/shard_map/ppermute | solution.py:665
  87.2 5.3 %collective-permute-done.7 = bf16[2,112,384]{2,1,0:T(8,128)(2,1)S(1)} collective-permute-done((bf16[2,112,384]{2,1,0:T(8,128)(2,1)S(1)}, bf16[2,112,384]{2,1,0:T(8,128)(2,1)S(1)}, u32[]{:S(2)}, u32[]{:S(2)}) %collective-permute-start.7) | collective-permute-done | bytes 172064 | tf_op jit(solution)/shard_map/ppermute | solution.py:665
  92.6 1.6 %convert_add_fusion.1 = f32[1,2,768,384]{3,2,1,0:T(8,128)} fusion(bf16[1,2,768,384]{3,2,1,0:T(8,128)(2,1)S(1)} %collective-permute-done.13, bf16[1,2,768,384]{3,2,1,0:T(8,128)(2,1)S(1)} %get-tuple-element.83), kind=kLoop, calls=%fused_computation.1 | loop fusion | flops 1769472 | bytes 4718592 | tf_op jit(solution)/shard_map/add | solution.py:774
  94.3 3.0 %convert_add_fusion = f32[1,2,192,3072]{3,2,1,0:T(8,128)} fusion(bf16[1,2,192,3072]{3,2,1,0:T(8,128)(2,1)S(1)} %collective-permute-done.12, bf16[1,2,192,3072]{3,2,1,0:T(8,128)(2,1)S(1)} %get-tuple-element.81), kind=kLoop, calls=%fused_computation | loop fusion | flops 3538944 | bytes 9437184 | tf_op jit(solution)/shard_map/add | solution.py:773
  97.3 2.4 %collective-permute-done.11.b = bf16[1,160,384]{2,1,0:T(8,128)(2,1)S(1)} collective-permute-done((bf16[1,160,384]{2,1,0:T(8,128)(2,1)S(1)}, bf16[1,160,384]{2,1,0:T(8,128)(2,1)S(1)}, u32[]{:S(2)}, u32[]{:S(2)}) %collective-permute-start.11) | collective-permute-done | bytes 122912 | tf_op jit(solution)/shard_map/ppermute | solution.py:660
  99.7 0.8 finish.1
  (19 shorter events, 0.4 us)
Async XLA Ops:
  0.6 12.5 %collective-permute-start = (bf16[1,2,192,3072]{3,2,1,0:T(8,128)(2,1)}, bf16[1,2,192,3072]{3,2,1,0:T(8,128)(2,1)S(1)}, u32[]{:S(2)}, u32[]{:S(2)}) collective-permute-start(bf16[1,2,192,3072]{3,2,1,0:T(8,128)(2,1)} %bitcast.14), channel_id=1, source_target_pairs={{0,1},{1,0},{2,3},{3,2},{4,5},{5,4},{6,7},{7,6},{8,9},{9,8},{10,11... | collective-permute-start | bytes 7077896 | tf_op jit(solution)/shard_map/ppermute | solution.py:660
  3.0 27.5 %all-to-all-start = ((bf16[32,96,128]{2,1,0:T(8,128)(2,1)}), bf16[32,96,128]{2,1,0:T(8,128)(2,1)S(1)}, u32[]{:S(2)}, u32[]{:S(2)}) async-start(bf16[32,96,128]{2,1,0:T(8,128)(2,1)} %pack.1), calls=%async_computation | async-start | bytes 1572864 | tf_op jit(solution)/shard_map/all_to_all | solution.py:732
  10.0 20.6 %copy-start = (s32[256]{0:T(256)S(1)}, s32[256]{0:T(256)}, u32[]{:S(2)}) copy-start(s32[256]{0:T(256)} %refs_1_.1) | copy-start | bytes 3076
  10.0 20.6 %copy-start.1 = (s32[32,1]{0,1:T(1,128)S(1)}, s32[32,1]{0,1:T(1,128)}, u32[]{:S(2)}) copy-start(s32[32,1]{0,1:T(1,128)} %param.12) | copy-start | bytes 388
  10.0 3.1 %collective-permute-start.1 = (bf16[1,2,768,384]{3,2,1,0:T(8,128)(2,1)}, bf16[1,2,768,384]{3,2,1,0:T(8,128)(2,1)S(1)}, u32[]{:S(2)}, u32[]{:S(2)}) collective-permute-start(bf16[1,2,768,384]{3,2,1,0:T(8,128)(2,1)} %bitcast.16), channel_id=1, source_target_pairs={{0,1},{1,0},{2,3},{3,2},{4,5},{5,4},{6,7},{7,6},{8,9},{9,8},{10,11... | collective-permute-start | bytes 3538952 | tf_op jit(solution)/shard_map/ppermute | solution.py:660
  54.4 4.2 %collective-permute-start.2 = (bf16[16,112,384]{2,1,0:T(8,128)(2,1)S(1)}, bf16[16,112,384]{2,1,0:T(8,128)(2,1)S(1)}, u32[]{:S(2)}, u32[]{:S(2)}) collective-permute-start(bf16[16,112,384]{2,1,0:T(8,128)(2,1)S(1)} %get-tuple-element.55), channel_id=1, source_target_pairs={{0,1},{1,0},{2,3},{3,2},{4,5},{5,4},{6,7},{7,6},{8,9},{9,8},{10,11... | collective-permute-start | bytes 4128776 | tf_op jit(solution)/shard_map/ppermute | solution.py:660
  54.5 4.0 %collective-permute-start.3 = (bf16[16,48,384]{2,1,0:T(8,128)(2,1)S(1)}, bf16[16,48,384]{2,1,0:T(8,128)(2,1)S(1)}, u32[]{:S(2)}, u32[]{:S(2)}) collective-permute-start(bf16[16,48,384]{2,1,0:T(8,128)(2,1)S(1)} %get-tuple-element.57), channel_id=1, source_target_pairs={{0,1},{1,0},{2,3},{3,2},{4,5},{5,4},{6,7},{7,6},{8,9},{9,8},{10,11... | collective-permute-start | bytes 1769480 | tf_op jit(solution)/shard_map/ppermute | solution.py:660
  55.0 3.5 %collective-permute-start.4 = (f32[10,384]{1,0:T(8,128)S(1)}, f32[10,384]{1,0:T(8,128)S(1)}, u32[]{:S(2)}, u32[]{:S(2)}) collective-permute-start(f32[10,384]{1,0:T(8,128)S(1)} %get-tuple-element.66), channel_id=1, source_target_pairs={{0,1},{1,0},{2,3},{3,2},{4,5},{5,4},{6,7},{7,6},{8,9},{9,8},{10,11... | collective-permute-start | bytes 46088 | tf_op jit(solution)/shard_map/ppermute | solution.py:660
  59.0 18.6 %collective-permute-start.5 = (bf16[8,112,384]{2,1,0:T(8,128)(2,1)S(1)}, bf16[8,112,384]{2,1,0:T(8,128)(2,1)S(1)}, u32[]{:S(2)}, u32[]{:S(2)}) collective-permute-start(bf16[8,112,384]{2,1,0:T(8,128)(2,1)S(1)} %get-tuple-element.67), channel_id=1, source_target_pairs={{0,2},{1,5},{2,0},{3,7},{4,6},{5,1},{6,4},{7,3},{8,10},{9,13},{10,... | collective-permute-start | bytes 2064392 | tf_op jit(solution)/shard_map/ppermute | solution.py:665
  67.1 27.2 %collective-permute-start.12 = (bf16[1,2,192,3072]{3,2,1,0:T(8,128)(2,1)S(1)}, bf16[1,2,192,3072]{3,2,1,0:T(8,128)(2,1)S(1)}, u32[]{:S(2)}, u32[]{:S(2)}) collective-permute-start(bf16[1,2,192,3072]{3,2,1,0:T(8,128)(2,1)S(1)} %get-tuple-element.82), channel_id=1, source_target_pairs={{0,1},{1,0},{2,3},{3,2},{4,5},{5,4},{6,7},{7,6},{8,9},{9,8},{10,11... | collective-permute-start | bytes 7077896 | tf_op jit(solution)/shard_map/ppermute | solution.py:660
  67.1 9.4 %collective-permute-start.8 = (bf16[8,48,384]{2,1,0:T(8,128)(2,1)S(1)}, bf16[8,48,384]{2,1,0:T(8,128)(2,1)S(1)}, u32[]{:S(2)}, u32[]{:S(2)}) collective-permute-start(bf16[8,48,384]{2,1,0:T(8,128)(2,1)S(1)} %get-tuple-element.68), channel_id=1, source_target_pairs={{0,8},{1,9},{2,10},{3,11},{4,12},{5,13},{6,14},{7,15},{8,0},{9,1},... | collective-permute-start | bytes 884744 | tf_op jit(solution)/shard_map/ppermute | solution.py:665
  67.9 24.7 %collective-permute-start.13 = (bf16[1,2,768,384]{3,2,1,0:T(8,128)(2,1)S(1)}, bf16[1,2,768,384]{3,2,1,0:T(8,128)(2,1)S(1)}, u32[]{:S(2)}, u32[]{:S(2)}) collective-permute-start(bf16[1,2,768,384]{3,2,1,0:T(8,128)(2,1)S(1)} %get-tuple-element.84), channel_id=1, source_target_pairs={{0,1},{1,0},{2,3},{3,2},{4,5},{5,4},{6,7},{7,6},{8,9},{9,8},{10,11... | collective-permute-start | bytes 3538952 | tf_op jit(solution)/shard_map/ppermute | solution.py:660
  76.6 5.4 %collective-permute-start.9 = (bf16[4,48,384]{2,1,0:T(8,128)(2,1)S(1)}, bf16[4,48,384]{2,1,0:T(8,128)(2,1)S(1)}, u32[]{:S(2)}, u32[]{:S(2)}) collective-permute-start(bf16[4,48,384]{2,1,0:T(8,128)(2,1)S(1)} %get-tuple-element.103), channel_id=1, source_target_pairs={{0,2},{1,3},{2,0},{3,1},{4,6},{5,7},{6,4},{7,5},{8,10},{9,11},{10,... | collective-permute-start | bytes 442376 | tf_op jit(solution)/shard_map/ppermute | solution.py:665
  77.8 8.1 %collective-permute-start.6 = (bf16[4,112,384]{2,1,0:T(8,128)(2,1)S(1)}, bf16[4,112,384]{2,1,0:T(8,128)(2,1)S(1)}, u32[]{:S(2)}, u32[]{:S(2)}) collective-permute-start(bf16[4,112,384]{2,1,0:T(8,128)(2,1)S(1)} %get-tuple-element.97), channel_id=1, source_target_pairs={{0,4},{1,9},{2,6},{3,11},{4,0},{5,13},{6,2},{7,15},{8,12},{9,1},{1... | collective-permute-start | bytes 1032200 | tf_op jit(solution)/shard_map/ppermute | solution.py:665
  82.1 5.1 %collective-permute-start.10 = (bf16[2,48,384]{2,1,0:T(8,128)(2,1)S(1)}, bf16[2,48,384]{2,1,0:T(8,128)(2,1)S(1)}, u32[]{:S(2)}, u32[]{:S(2)}) collective-permute-start(bf16[2,48,384]{2,1,0:T(8,128)(2,1)S(1)} %get-tuple-element.107), channel_id=1, source_target_pairs={{0,4},{1,5},{2,6},{3,7},{4,0},{5,1},{6,2},{7,3},{8,12},{9,13},{10,... | collective-permute-start | bytes 221192 | tf_op jit(solution)/shard_map/ppermute | solution.py:665
  86.0 6.5 %collective-permute-start.7 = (bf16[2,112,384]{2,1,0:T(8,128)(2,1)S(1)}, bf16[2,112,384]{2,1,0:T(8,128)(2,1)S(1)}, u32[]{:S(2)}, u32[]{:S(2)}) collective-permute-start(bf16[2,112,384]{2,1,0:T(8,128)(2,1)S(1)} %get-tuple-element.101), channel_id=1, source_target_pairs={{0,8},{1,3},{2,10},{3,1},{4,12},{5,7},{6,14},{7,5},{8,0},{9,11},{1... | collective-permute-start | bytes 516104 | tf_op jit(solution)/shard_map/ppermute | solution.py:665
  92.5 7.2 %collective-permute-start.11 = (bf16[1,160,384]{2,1,0:T(8,128)(2,1)S(1)}, bf16[1,160,384]{2,1,0:T(8,128)(2,1)S(1)}, u32[]{:S(2)}, u32[]{:S(2)}) collective-permute-start(bf16[1,160,384]{2,1,0:T(8,128)(2,1)S(1)} %pad_maximum_fusion), channel_id=1, source_target_pairs={{0,16},{1,17},{2,18},{3,19},{4,20},{5,21},{6,22},{7,23},{8,24},{9,... | collective-permute-start | bytes 368648 | tf_op jit(solution)/shard_map/ppermute | solution.py:660
